TPU v7x, 32 devices: a whole 2x2x4 slice. The times are simulated.
32 devices in a mesh: groups: 2 (over x), sp: 8 (over z, y), fsdp: 2 (over core).
Axes of the slice: x: 2, y: 2, z: 4, core: 2. Of those that a mesh axis runs over, the one named last changes fastest.
Arguments:
- policy_hidden: bfloat16 [4, 256, 4096], P(('groups', 'fsdp'), 'sp'), parts along dimension 0, may hold values from -6 to 6
- policy_queries: bfloat16 [4, 256, 1024], P(('groups', 'fsdp'), 'sp'), parts along dimension 0, may hold values from -512 to 512
- policy_documents: int32 [4, 256], P(('groups', 'fsdp'), 'sp'), parts along dimension 0, may hold values from 0 to 31, never falling along the last dimension, each value on 1 to 128 neighbouring positions
- policy_gain: bfloat16 [4096], P(('sp', 'fsdp')), may hold values from 0.099609375 to 1.8984375
- policy_key_weight: bfloat16 [4096, 512], P(('sp', 'fsdp')), may hold values from -0.09375 to 0.09375
- policy_value_weight: bfloat16 [4096, 512], P(('sp', 'fsdp')), may hold values from -0.09375 to 0.09375
- frozen_hidden: bfloat16 [4, 256, 4096], P(('groups', 'fsdp'), 'sp'), parts along dimension 0, may hold values from -6 to 6
- frozen_queries: bfloat16 [4, 256, 1024], P(('groups', 'fsdp'), 'sp'), parts along dimension 0, may hold values from -512 to 512
- frozen_documents: int32 [4, 256], P(('groups', 'fsdp'), 'sp'), parts along dimension 0, may hold values from 0 to 31, never falling along the last dimension, each value on 1 to 128 neighbouring positions
- frozen_gain: bfloat16 [4096], P(('sp', 'fsdp')), may hold values from 0.099609375 to 1.8984375
- frozen_key_weight: bfloat16 [4096, 512], P(('sp', 'fsdp')), may hold values from -0.09375 to 0.09375
- frozen_value_weight: bfloat16 [4096, 512], P(('sp', 'fsdp')), may hold values from -0.09375 to 0.09375
Outputs:
- policy_mixed: bfloat16 [4, 256, 1024], P(('groups', 'fsdp'), 'sp'), parts along dimension 0
- frozen_mixed: bfloat16 [4, 256, 1024], P(('groups', 'fsdp'), 'sp'), parts along dimension 0
There are 2 independent parts, one for each index of `groups`. A program takes and returns all parts, laid end to end along the dimension named above; an argument that names none is the same for every part. Nothing has to cross between parts.
Inputs may be any that keep to these rules, and one draw needn't show every extreme that they name: `policy_documents`: along each sequence the ids never fall, and each document holds 1 to 128 positions. `frozen_documents`: along each sequence the ids never fall, and each document holds 1 to 128 positions.
All inputs are finite; a program needn't handle non-finite values.
Results may differ from a plain program's by a relative error of at most 0.007.
The roundings to bfloat16 on the way count: a program that leaves them out, or rounds other values in their place, can miss the bound.
Values may be sent and summed in bfloat16 or wider, within the bound.
A program may use at most 128 MiB of HBM per device.

v0:
```python
import jax
import jax.numpy as jnp
from jax import lax
from jax.sharding import PartitionSpec as P

HEAD_DIM = 128


EPS = 1e-05
ROPE_BASE = 500000.0
MASKED = -1e30


def rotate(raw_keys, positions):
    half_dim = HEAD_DIM // 2
    frequency = jnp.exp(
        -jnp.log(ROPE_BASE) * jnp.arange(half_dim, dtype=jnp.float32) * 2.0 / HEAD_DIM
    )
    angles = positions.astype(jnp.float32)[:, None] * frequency[None, :]
    cosines = jnp.cos(angles)[:, None, :]
    sines = jnp.sin(angles)[:, None, :]
    front_half = raw_keys[..., :half_dim]
    back_half = raw_keys[..., half_dim:]
    return jnp.concatenate(
        [front_half * cosines - back_half * sines, back_half * cosines + front_half * sines],
        axis=-1,
    )


def project(hidden, gain, key_weight, value_weight):
    tokens = hidden.shape[1]
    widened = hidden[0].astype(jnp.float32)
    inverse = lax.rsqrt(jnp.mean(widened * widened, axis=-1, keepdims=True) + EPS)
    scaled = widened * inverse
    gain_rows = lax.all_gather(gain, ("sp", "fsdp"), axis=0, tiled=True)
    key_rows = lax.all_gather(key_weight, ("sp", "fsdp"), axis=0, tiled=True)
    value_rows = lax.all_gather(value_weight, ("sp", "fsdp"), axis=0, tiled=True)
    normed = (scaled * gain_rows.astype(jnp.float32)[None, :]).astype(jnp.bfloat16)
    raw_keys = jnp.dot(normed, key_rows, preferred_element_type=jnp.float32)
    raw_values = jnp.dot(normed, value_rows, preferred_element_type=jnp.float32)
    positions = lax.axis_index("sp") * tokens + jnp.arange(tokens, dtype=jnp.int32)
    key_heads = rotate(raw_keys.reshape(tokens, -1, HEAD_DIM), positions).astype(jnp.bfloat16)
    value_heads = raw_values.astype(jnp.bfloat16).reshape(tokens, -1, HEAD_DIM)
    return (key_heads, value_heads)


def attend(queries, key_heads, value_heads, documents):
    length = queries.shape[0]
    head_count = queries.shape[1]
    block_rows = min(512, length)
    margin = min(512, length // 2)
    window = block_rows + margin
    factor = HEAD_DIM ** (-0.5)
    offsets = jnp.arange(block_rows, dtype=jnp.int32)
    window_offsets = jnp.arange(window, dtype=jnp.int32)
    padding = jnp.zeros((margin, head_count, HEAD_DIM), jnp.bfloat16)
    padded_keys = jnp.concatenate([padding, key_heads], axis=0)
    padded_values = jnp.concatenate([padding, value_heads], axis=0)
    padded_docs = jnp.concatenate([jnp.full((margin,), -1, jnp.int32), documents], axis=0)

    def one_block(block_index):
        first = block_index * block_rows
        query_block = lax.dynamic_slice_in_dim(queries, first, block_rows, 0)
        query_docs = lax.dynamic_slice_in_dim(documents, first, block_rows, 0)
        query_positions = first + offsets
        key_block = lax.dynamic_slice_in_dim(padded_keys, first, window, 0)
        value_block = lax.dynamic_slice_in_dim(padded_values, first, window, 0)
        key_docs = lax.dynamic_slice_in_dim(padded_docs, first, window, 0)
        key_positions = first - margin + window_offsets
        allowed = (key_positions[None, :] <= query_positions[:, None]) & (
            key_docs[None, :] == query_docs[:, None]
        )
        scores = (
            jnp.einsum("qnd,knd->nqk", query_block, key_block, preferred_element_type=jnp.float32)
            * factor
        )
        scores = jnp.where(allowed[None], scores, MASKED)
        highest = jnp.max(scores, axis=-1, keepdims=True)
        exponent = jnp.where(allowed[None], jnp.exp(scores - highest), 0.0)
        weights = (exponent / jnp.sum(exponent, axis=-1, keepdims=True)).astype(jnp.bfloat16)
        blended = jnp.einsum(
            "nqk,knd->qnd", weights, value_block, preferred_element_type=jnp.float32
        )
        return blended.astype(jnp.bfloat16)

    blocks = lax.map(one_block, jnp.arange(length // block_rows, dtype=jnp.int32))
    return blocks.reshape(length, head_count, HEAD_DIM)


def run_model(hidden, queries, documents, gain, key_weight, value_weight):
    tokens = hidden.shape[1]
    head_count = queries.shape[2] // HEAD_DIM
    query_local = queries[0].reshape(tokens, head_count, HEAD_DIM)
    every_doc = lax.all_gather(documents[0], "sp", axis=0, tiled=True)
    key_heads, value_heads = project(hidden, gain, key_weight, value_weight)
    group_size = head_count // key_heads.shape[1]
    wide_keys = jnp.repeat(key_heads, group_size, axis=1)
    wide_values = jnp.repeat(value_heads, group_size, axis=1)
    query_spread, key_spread, value_spread = (
        lax.all_to_all(query_local, "sp", split_axis=1, concat_axis=0, tiled=True),
        lax.all_to_all(wide_keys, "sp", split_axis=1, concat_axis=0, tiled=True),
        lax.all_to_all(wide_values, "sp", split_axis=1, concat_axis=0, tiled=True),
    )
    mixed = attend(query_spread, key_spread, value_spread, every_doc)
    returned = lax.all_to_all(mixed, "sp", split_axis=0, concat_axis=1, tiled=True)
    return returned.reshape(1, tokens, head_count * HEAD_DIM)


def per_device(
    policy_hidden,
    policy_queries,
    policy_documents,
    policy_gain,
    policy_key_weight,
    policy_value_weight,
    frozen_hidden,
    frozen_queries,
    frozen_documents,
    frozen_gain,
    frozen_key_weight,
    frozen_value_weight,
):
    policy_mixed = run_model(
        policy_hidden,
        policy_queries,
        policy_documents,
        policy_gain,
        policy_key_weight,
        policy_value_weight,
    )
    frozen_mixed = run_model(
        frozen_hidden,
        frozen_queries,
        frozen_documents,
        frozen_gain,
        frozen_key_weight,
        frozen_value_weight,
    )
    return (policy_mixed, frozen_mixed)


def solution(mesh):
    return jax.shard_map(
        per_device,
        mesh=mesh,
        in_specs=(
            P(("groups", "fsdp"), "sp", None),
            P(("groups", "fsdp"), "sp", None),
            P(("groups", "fsdp"), "sp"),
            P(("sp", "fsdp")),
            P(("sp", "fsdp"), None),
            P(("sp", "fsdp"), None),
            P(("groups", "fsdp"), "sp", None),
            P(("groups", "fsdp"), "sp", None),
            P(("groups", "fsdp"), "sp"),
            P(("sp", "fsdp")),
            P(("sp", "fsdp"), None),
            P(("sp", "fsdp"), None),
        ),
        out_specs=(P(("groups", "fsdp"), "sp", None), P(("groups", "fsdp"), "sp", None)),
        check_vma=False,
    )
```

profile of v0, /device:TPU:0, one launch (start us, length us, event | category | flops | bytes accessed | tf_op | source)
XLA Modules:
  0.0 280.7 jit_solution(6077862936525834880)
XLA Ops:
  11.5 7.3 %all-to-all-start.6 = ((bf16[32,8,128]{2,0,1:T(8,128)(2,1)}), bf16[32,8,128]{2,0,1:T(8,128)(2,1)S(1)}, u32[]{:S(2)}, u32[]{:S(2)}) async-start(bf16[32,8,128]{2,0,1:T(8,128)(2,1)} %copy.43), calls=%async_computation.6 | async-start | bytes 131072 | tf_op jit(solution)/shard_map/all_to_all | solution.py:100
  19.4 21.8 %all-gather.3 = bf16[16,1,256]{2,1,0:T(2,128)(2,1)S(1)} all-gather(bf16[1,1,256]{2,1,0:T(2,128)(2,1)S(1)} %reshape.242), channel_id=1, replica_groups=mesh['groups'=2,'sp'=8,'fsdp'=2] {'sp','fsdp'}, dimensions={0}, use_global_device_ids=true | all-gather | bytes 8704 | tf_op jit(solution)/shard_map/all_gather | solution.py:35
  41.9 17.8 %all-gather.2 = bf16[16,1,256]{2,1,0:T(2,128)(2,1)S(1)} all-gather(bf16[1,1,256]{2,1,0:T(2,128)(2,1)S(1)} %reshape.240), channel_id=1, replica_groups=mesh['groups'=2,'sp'=8,'fsdp'=2] {'sp','fsdp'}, dimensions={0}, use_global_device_ids=true | all-gather | bytes 8704 | tf_op jit(solution)/shard_map/all_gather | solution.py:35
  63.1 8.1 %all-reduce.8 = (s32[256]{0:T(256)S(1)}, s32[256]{0:T(256)S(1)}) all-reduce(s32[256]{0:T(256)S(1)} %bitcast_dynamic-update-slice_fusion.1, s32[256]{0:T(256)S(1)} %bitcast_dynamic-update-slice_fusion), channel_id=2, replica_groups=mesh['groups'=2,'sp'=8,'fsdp'=2] {'sp'}, use_global_device_ids=true, to_apply=%add.6 | all-reduce | flops 512 | bytes 4096 | tf_op jit(solution)/shard_map/all_gather | solution.py:94
  75.2 6.4 %copy.42 = bf16[512,4096]{1,0:T(8,128)(2,1)} copy(bf16[512,4096]{0,1:T(8,128)(2,1)} %bitcast.149) | data formatting | bytes 8388608 | tf_op jit(solution)/shard_map/dot_general | solution.py:39
  81.6 33.1 %all-gather.11.cloned.1.call-done = bf16[4096,512]{1,0:T(8,128)(2,1)} async-done(((bf16[256,512]{1,0:T(8,128)(2,1)}), bf16[4096,512]{1,0:T(8,128)(2,1)}) %all-gather.11.cloned.1.call-update) | async-done | bytes 4194320 | tf_op jit(solution)/shard_map/all_gather | solution.py:36
  114.6 6.4 %copy.37 = bf16[512,4096]{1,0:T(8,128)(2,1)} copy(bf16[512,4096]{0,1:T(8,128)(2,1)} %bitcast.150) | data formatting | bytes 8388608 | tf_op jit(solution)/shard_map/dot_general | solution.py:39
  121.1 3.8 %fusion.25 = f32[32,4,128]{2,0,1:T(8,128)S(1)} fusion(bf16[4,128,4096]{2,1,0:T(8,128)(2,1)} %bitcast.147, bf16[1,32,4096]{2,1,0:T(8,128)(2,1)S(1)} %copy-done.1, f32[4096]{0:T(1024)S(1)} %bitcast.157, f32[32]{0:T(128)S(1)} %add_rsqrt_fusion), kind=kOutput, calls=%fused_computation.40 | convolution fusion | flops 134742016 | bytes 4538496 | tf_op jit(solution)/shard_map/dot_general | solution.py:39
  126.3 39.6 %all-gather.13.cloned.1.call-done = bf16[4096,512]{1,0:T(8,128)(2,1)} async-done(((bf16[256,512]{1,0:T(8,128)(2,1)}), bf16[4096,512]{1,0:T(8,128)(2,1)}) %all-gather.13.cloned.1.call-update) | async-done | bytes 4194320 | tf_op jit(solution)/shard_map/all_gather | solution.py:37
  165.9 3.1 %fusion.7 = bf16[4,4,8,128]{3,2,1,0:T(8,128)(2,1)S(1)} fusion(bf16[4096,512]{1,0:T(8,128)(2,1)} %all-gather.13.cloned.1.call-done, bf16[1,32,4096]{2,1,0:T(8,128)(2,1)S(1)} %copy-done.1, f32[4096]{0:T(1024)S(1)} %bitcast.158, f32[32]{0:T(128)S(1)} %add_rsqrt_fusion), kind=kOutput, calls=%fused_computation.13 | convolution fusion | flops 134758400 | bytes 4505728 | tf_op jit(solution)/shard_map/dot_general | solution.py:40
  169.0 3.4 %all-to-all-start.2 = ((bf16[32,8,128]{2,0,1:T(8,128)(2,1)}), bf16[32,8,128]{2,0,1:T(8,128)(2,1)S(1)}, u32[]{:S(2)}, u32[]{:S(2)}) async-start(bf16[32,8,128]{2,0,1:T(8,128)(2,1)} %copy.38), calls=%async_computation.2 | async-start | bytes 131072 | tf_op jit(solution)/shard_map/all_to_all | solution.py:100
  172.5 6.7 %all-to-all-done.2 = bf16[32,8,128]{2,0,1:T(8,128)(2,1)S(1)} async-done(((bf16[32,8,128]{2,0,1:T(8,128)(2,1)}), bf16[32,8,128]{2,0,1:T(8,128)(2,1)S(1)}, u32[]{:S(2)}, u32[]{:S(2)}) %all-to-all-start.2) | async-done | bytes 65568 | tf_op jit(solution)/shard_map/all_to_all | solution.py:100
  179.9 3.4 %all-to-all-start.5 = ((bf16[32,8,128]{2,0,1:T(8,128)(2,1)}), bf16[32,8,128]{2,0,1:T(8,128)(2,1)S(1)}, u32[]{:S(2)}, u32[]{:S(2)}) async-start(bf16[32,8,128]{2,0,1:T(8,128)(2,1)} %bitcast.37), calls=%async_computation.5 | async-start | bytes 131072 | tf_op jit(solution)/shard_map/all_to_all | solution.py:101
  183.3 34.1 %all-gather.9.cloned.1.call-done = bf16[4096,512]{1,0:T(8,128)(2,1)} async-done(((bf16[256,512]{1,0:T(8,128)(2,1)}), bf16[4096,512]{1,0:T(8,128)(2,1)}) %all-gather.9.cloned.1.call-update) | async-done | bytes 4194320 | tf_op jit(solution)/shard_map/all_gather | solution.py:37
  221.1 3.4 %all-to-all-start.1 = ((bf16[32,8,128]{2,0,1:T(8,128)(2,1)}), bf16[32,8,128]{2,0,1:T(8,128)(2,1)S(1)}, u32[]{:S(2)}, u32[]{:S(2)}) async-start(bf16[32,8,128]{2,0,1:T(8,128)(2,1)} %bitcast.13), calls=%async_computation.1 | async-start | bytes 131072 | tf_op jit(solution)/shard_map/all_to_all | solution.py:101
  224.7 6.6 %all-to-all-done.1 = bf16[32,8,128]{2,0,1:T(8,128)(2,1)S(1)} async-done(((bf16[32,8,128]{2,0,1:T(8,128)(2,1)}), bf16[32,8,128]{2,0,1:T(8,128)(2,1)S(1)}, u32[]{:S(2)}, u32[]{:S(2)}) %all-to-all-start.1) | async-done | bytes 65568 | tf_op jit(solution)/shard_map/all_to_all | solution.py:101
  231.9 3.4 %all-to-all-start.4 = ((bf16[32,8,128]{2,0,1:T(8,128)(2,1)}), bf16[32,8,128]{2,0,1:T(8,128)(2,1)S(1)}, u32[]{:S(2)}, u32[]{:S(2)}) async-start(bf16[32,8,128]{2,0,1:T(8,128)(2,1)} %bitcast.27), calls=%async_computation.4 | async-start | bytes 131072 | tf_op jit(solution)/shard_map/all_to_all | solution.py:102
  235.9 6.3 %all-to-all-done.4 = bf16[32,8,128]{2,0,1:T(8,128)(2,1)S(1)} async-done(((bf16[32,8,128]{2,0,1:T(8,128)(2,1)}), bf16[32,8,128]{2,0,1:T(8,128)(2,1)S(1)}, u32[]{:S(2)}, u32[]{:S(2)}) %all-to-all-start.4) | async-done | bytes 65568 | tf_op jit(solution)/shard_map/all_to_all | solution.py:102
  242.8 3.4 %all-to-all-start = ((bf16[32,8,128]{2,0,1:T(8,128)(2,1)}), bf16[32,8,128]{2,0,1:T(8,128)(2,1)S(1)}, u32[]{:S(2)}, u32[]{:S(2)}) async-start(bf16[32,8,128]{2,0,1:T(8,128)(2,1)} %bitcast.2), calls=%async_computation | async-start | bytes 131072 | tf_op jit(solution)/shard_map/all_to_all | solution.py:102
  248.4 4.6 %all-to-all-done = bf16[32,8,128]{2,0,1:T(8,128)(2,1)S(1)} async-done(((bf16[32,8,128]{2,0,1:T(8,128)(2,1)}), bf16[32,8,128]{2,0,1:T(8,128)(2,1)S(1)}, u32[]{:S(2)}, u32[]{:S(2)}) %all-to-all-start) | async-done | bytes 65568 | tf_op jit(solution)/shard_map/all_to_all | solution.py:102
  253.0 3.3 %all-to-all-start.7 = ((bf16[8,2,2048]{2,1,0:T(2,128)(2,1)}), bf16[8,2,2048]{2,1,0:T(2,128)(2,1)S(1)}, u32[]{:S(2)}, u32[]{:S(2)}) async-start(bf16[8,2,2048]{2,1,0:T(2,128)(2,1)} %reshape.256), calls=%async_computation.7 | async-start | bytes 131072 | tf_op jit(solution)/shard_map/all_to_all | solution.py:105
  258.1 5.1 %all-to-all-done.7 = bf16[8,2,2048]{2,1,0:T(2,128)(2,1)S(1)} async-done(((bf16[8,2,2048]{2,1,0:T(2,128)(2,1)}), bf16[8,2,2048]{2,1,0:T(2,128)(2,1)S(1)}, u32[]{:S(2)}, u32[]{:S(2)}) %all-to-all-start.7) | async-done | bytes 65568 | tf_op jit(solution)/shard_map/all_to_all | solution.py:105
  263.2 3.4 %all-to-all-start.3 = ((bf16[8,2,2048]{2,1,0:T(2,128)(2,1)}), bf16[8,2,2048]{2,1,0:T(2,128)(2,1)S(1)}, u32[]{:S(2)}, u32[]{:S(2)}) async-start(bf16[8,2,2048]{2,1,0:T(2,128)(2,1)} %reshape.254), calls=%async_computation.3 | async-start | bytes 131072 | tf_op jit(solution)/shard_map/all_to_all | solution.py:105
  267.3 6.1 %all-to-all-done.3 = bf16[8,2,2048]{2,1,0:T(2,128)(2,1)S(1)} async-done(((bf16[8,2,2048]{2,1,0:T(2,128)(2,1)}), bf16[8,2,2048]{2,1,0:T(2,128)(2,1)S(1)}, u32[]{:S(2)}, u32[]{:S(2)}) %all-to-all-start.3) | async-done | bytes 65568 | tf_op jit(solution)/shard_map/all_to_all | solution.py:105
  (70 shorter events, 25.8 us)
Async XLA Ops:
  7.2 68.0 %all-gather.15.cloned.1.call-start = ((), (), s32[]{:S(2)}) async-start(), calls=%async_computation.11 | async-start | bytes 4456448 | tf_op jit(solution)/shard_map/all_gather | solution.py:36
  7.9 106.7 %all-gather.11.cloned.1.call-start = ((), (), s32[]{:S(2)}) async-start(), calls=%async_computation.9 | async-start | bytes 4456448 | tf_op jit(solution)/shard_map/all_gather | solution.py:36
  8.6 157.2 %all-gather.13.cloned.1.call-start = ((), (), s32[]{:S(2)}) async-start(), calls=%async_computation.10 | async-start | bytes 4456448 | tf_op jit(solution)/shard_map/all_gather | solution.py:37
  9.4 208.0 %all-gather.9.cloned.1.call-start = ((), (), s32[]{:S(2)}) async-start(), calls=%async_computation.8 | async-start | bytes 4456448 | tf_op jit(solution)/shard_map/all_gather | solution.py:37
  11.5 157.5 %all-to-all-start.6 = ((bf16[32,8,128]{2,0,1:T(8,128)(2,1)}), bf16[32,8,128]{2,0,1:T(8,128)(2,1)S(1)}, u32[]{:S(2)}, u32[]{:S(2)}) async-start(bf16[32,8,128]{2,0,1:T(8,128)(2,1)} %copy.43), calls=%async_computation.6 | async-start | bytes 131072 | tf_op jit(solution)/shard_map/all_to_all | solution.py:100
  114.6 6.4 %copy-start.1 = (bf16[1,32,4096]{2,1,0:T(8,128)(2,1)S(1)}, bf16[1,32,4096]{2,1,0:T(8,128)(2,1)}, u32[]{:S(2)}) copy-start(bf16[1,32,4096]{2,1,0:T(8,128)(2,1)} %param.18) | copy-start | bytes 786436
  121.1 3.8 %copy-start = (bf16[512,4096]{1,0:T(8,128)(2,1)S(1)}, bf16[512,4096]{1,0:T(8,128)(2,1)}, u32[]{:S(2)}) copy-start(bf16[512,4096]{1,0:T(8,128)(2,1)} %copy.37) | copy-start | bytes 12582916
  121.1 3.9 %copy-start.2 = (bf16[1,32,4096]{2,1,0:T(8,128)(2,1)S(1)}, bf16[1,32,4096]{2,1,0:T(8,128)(2,1)}, u32[]{:S(2)}) copy-start(bf16[1,32,4096]{2,1,0:T(8,128)(2,1)} %param.12) | copy-start | bytes 786436
  169.0 10.3 %all-to-all-start.2 = ((bf16[32,8,128]{2,0,1:T(8,128)(2,1)}), bf16[32,8,128]{2,0,1:T(8,128)(2,1)S(1)}, u32[]{:S(2)}, u32[]{:S(2)}) async-start(bf16[32,8,128]{2,0,1:T(8,128)(2,1)} %copy.38), calls=%async_computation.2 | async-start | bytes 131072 | tf_op jit(solution)/shard_map/all_to_all | solution.py:100
  179.9 40.5 %all-to-all-start.5 = ((bf16[32,8,128]{2,0,1:T(8,128)(2,1)}), bf16[32,8,128]{2,0,1:T(8,128)(2,1)S(1)}, u32[]{:S(2)}, u32[]{:S(2)}) async-start(bf16[32,8,128]{2,0,1:T(8,128)(2,1)} %bitcast.37), calls=%async_computation.5 | async-start | bytes 131072 | tf_op jit(solution)/shard_map/all_to_all | solution.py:101
  221.1 10.2 %all-to-all-start.1 = ((bf16[32,8,128]{2,0,1:T(8,128)(2,1)}), bf16[32,8,128]{2,0,1:T(8,128)(2,1)S(1)}, u32[]{:S(2)}, u32[]{:S(2)}) async-start(bf16[32,8,128]{2,0,1:T(8,128)(2,1)} %bitcast.13), calls=%async_computation.1 | async-start | bytes 131072 | tf_op jit(solution)/shard_map/all_to_all | solution.py:101
  231.9 10.2 %all-to-all-start.4 = ((bf16[32,8,128]{2,0,1:T(8,128)(2,1)}), bf16[32,8,128]{2,0,1:T(8,128)(2,1)S(1)}, u32[]{:S(2)}, u32[]{:S(2)}) async-start(bf16[32,8,128]{2,0,1:T(8,128)(2,1)} %bitcast.27), calls=%async_computation.4 | async-start | bytes 131072 | tf_op jit(solution)/shard_map/all_to_all | solution.py:102
  242.8 10.2 %all-to-all-start = ((bf16[32,8,128]{2,0,1:T(8,128)(2,1)}), bf16[32,8,128]{2,0,1:T(8,128)(2,1)S(1)}, u32[]{:S(2)}, u32[]{:S(2)}) async-start(bf16[32,8,128]{2,0,1:T(8,128)(2,1)} %bitcast.2), calls=%async_computation | async-start | bytes 131072 | tf_op jit(solution)/shard_map/all_to_all | solution.py:102
  253.0 10.2 %all-to-all-start.7 = ((bf16[8,2,2048]{2,1,0:T(2,128)(2,1)}), bf16[8,2,2048]{2,1,0:T(2,128)(2,1)S(1)}, u32[]{:S(2)}, u32[]{:S(2)}) async-start(bf16[8,2,2048]{2,1,0:T(2,128)(2,1)} %reshape.256), calls=%async_computation.7 | async-start | bytes 131072 | tf_op jit(solution)/shard_map/all_to_all | solution.py:105
  263.2 10.2 %all-to-all-start.3 = ((bf16[8,2,2048]{2,1,0:T(2,128)(2,1)}), bf16[8,2,2048]{2,1,0:T(2,128)(2,1)S(1)}, u32[]{:S(2)}, u32[]{:S(2)}) async-start(bf16[8,2,2048]{2,1,0:T(2,128)(2,1)} %reshape.254), calls=%async_computation.3 | async-start | bytes 131072 | tf_op jit(solution)/shard_map/all_to_all | solution.py:105
Sparse Core Ops, SparseCore 0:
  10.1 53.3 all-gather.14
  65.7 48.9 all-gather.10
  116.8 49.0 all-gather.12
  167.9 49.4 all-gather.8
where the time goes:
time: 282 us; the launch traced here: 281 us
  waiting for transfers between devices  145 us (51%)
  blocking collectives  47.7 us (17%)
  starting transfers between devices  30.9 us (11%)
  local copies, waits for them, and re-layouts  26 us (9%)
  between operations  14.7 us (5%)
  matrix products  12.5 us (4%)
  other arithmetic  4.27 us (2%)
    all_gather x2, waiting for transfers between devices, project(): lax.all_gather(value_weight, ('sp', 'fsdp'), axis=0, tiled=True)  73.7 us
    all_gather x2, blocking collectives, project(): gain_rows = lax.all_gather(gain, ('sp', 'fsdp'), axis=0, tiled=True)  39.6 us
    all_gather x2, waiting for transfers between devices, project(): key_rows = lax.all_gather(key_weight, ('sp', 'fsdp'), axis=0, tiled=True)  33.1 us
    dot_general x2, local copies, waits for them, and re-layouts, project(): raw_keys = jnp.dot(normed, key_rows, preferred_element_type=jnp.float32)  12.8 us
    all_to_all x2, waiting for transfers between devices, run_model(): lax.all_to_all(mixed, 'sp', split_axis=0, concat_axis=1, tiled=True)  11.1 us
    all_to_all x2, waiting for transfers between devices, run_model(): lax.all_to_all(wide_values, 'sp', split_axis=1, concat_axis=0, tiled=True)  10.8 us
    all_to_all x2, starting transfers between devices, run_model(): lax.all_to_all(query_local, 'sp', split_axis=1, concat_axis=0, tiled=True)  10.7 us
    all_gather x1, blocking collectives, run_model(): every_doc = lax.all_gather(documents[0], 'sp', axis=0, tiled=True)  8.09 us
  transfers between devices with their start and end apart: 12, of which 9 were waited for; matrix products, arithmetic and copies ran while one was open for 14% of the time, Pallas kernels for 0%

commit v1 on v0

--- a/solution.py
+++ b/solution.py
@@ -1,6 +1,10 @@
+import functools
+
 import jax
 import jax.numpy as jnp
 from jax import lax
+from jax.experimental import pallas as pl
+from jax.experimental.pallas import tpu as pltpu
 from jax.sharding import PartitionSpec as P
 
 HEAD_DIM = 128
@@ -106,7 +110,305 @@
     return returned.reshape(1, tokens, head_count * HEAD_DIM)
 
 
+MESH = pl.DeviceIdType.MESH
+
+
+def fits(mesh, hidden, queries, key_weight):
+    sp, cores = mesh.shape["sp"], mesh.shape["fsdp"]
+    tokens = hidden.shape[1]
+    kv_heads = key_weight.shape[1] // HEAD_DIM
+    return (
+        cores == 2
+        and sp % 2 == 0
+        and kv_heads % 2 == 0
+        and sp // 2 == cores * (kv_heads // 2)
+        and queries.shape[2] % (kv_heads * HEAD_DIM) == 0
+        and key_weight.shape[0] % 128 == 0
+        and hidden.shape[2] == key_weight.shape[0] * sp * cores
+        and tokens % 16 == 0
+        and tokens <= 128
+    )
+
+
+def fused_kernel(
+    sp_count,
+    hidden0, hidden1, queries0, queries1, key0, key1, value0, value1,
+    gains, documents, cosines, sines,
+    out,
+    rows, wide_k, wide_v, gain_rows, norm_send, norm_rows, query_rows, doc_rows,
+    part_send, parts, doc_wide, mixed,
+    send_sem, hid_sem, fwd_sem, w_sem, gain_sem, norm_sem, q_sem, doc_sem, part_sem, out_sem,
+):
+    hiddens, queries = (hidden0, hidden1), (queries0, queries1)
+    keys, values = (key0, key1), (value0, value1)
+    tokens, features = hidden0.shape[1], key0.shape[0]
+    slab = 4 * features
+    half = key0.shape[1] // 2
+    per_half = half // HEAD_DIM
+    head_cols = query_rows.shape[1]
+    length = query_rows.shape[0]
+    layers = sp_count // 2
+    sp, core = lax.axis_index("sp"), lax.axis_index("fsdp")
+    z, y = sp // 2, sp % 2
+    me = sp * 2 + core
+    total = sp_count * 2
+
+    barrier = pltpu.get_barrier_semaphore()
+    for step in range(1, total):
+        other = lax.rem(me + step, total)
+        pl.semaphore_signal(
+            barrier, inc=1, device_id={"sp": other // 2, "fsdp": other % 2}, device_id_type=MESH
+        )
+
+    square = (
+        lax.broadcasted_iota(jnp.int32, (tokens, 128), 0)
+        == lax.broadcasted_iota(jnp.int32, (tokens, 128), 1)
+    )
+    for m in range(2):
+        wide = hiddens[m][0].astype(jnp.float32)
+        inverse = lax.rsqrt(jnp.mean(wide * wide, axis=-1, keepdims=True) + EPS)
+        norm_send[m] = jnp.sum(jnp.where(square, inverse, 0.0), axis=0, keepdims=True)
+
+    pl.semaphore_wait(barrier, total - 1)
+
+    pending = []
+
+    def remote(src, dst, recv, to_sp, to_core):
+        slot = len(pending)
+
+        def make():
+            return pltpu.make_async_remote_copy(
+                src_ref=src, dst_ref=dst, send_sem=send_sem.at[slot], recv_sem=recv,
+                device_id={"sp": to_sp, "fsdp": to_core}, device_id_type=MESH,
+            )
+
+        return make
+
+    def send(src, dst, recv, to_sp, to_core, own):
+        make = remote(src, dst, recv, to_sp, to_core)
+        if own is None:
+            pending.append((None, make))
+            make().start()
+            return
+        away = jnp.logical_not(own)
+        pending.append((away, make))
+
+        @pl.when(away)
+        def _():
+            make().start()
+
+        @pl.when(own)
+        def _():
+            pltpu.make_async_copy(src, dst, recv).start()
+
+    def arrive(dst, recv):
+        pltpu.make_async_copy(dst, dst, recv).wait()
+
+    for dz in range(layers):
+        to_z = lax.rem(z + dz, layers)
+        for m in range(2):
+            send(
+                hiddens[m].at[0, :, pl.ds(pl.multiple_of(to_z * slab, 128), slab)],
+                rows.at[sp, pl.ds(pl.multiple_of(core * tokens, 16), tokens)],
+                hid_sem.at[z, core],
+                to_z * 2 + y, m,
+                (core == m) if dz == 0 else None,
+            )
+    place = pl.ds(pl.multiple_of((y * 2 + core) * features, 128), features)
+    for dy in (1, 0):
+        to_y = (y + dy) % 2
+        columns = pl.ds(pl.multiple_of(to_y * half, 128), half)
+        for m in range(2):
+            own = (core == m) if dy == 0 else None
+            send(gains.at[m], gain_rows.at[y * 2 + core], gain_sem.at[y * 2 + core], z * 2 + to_y, m, own)
+            send(keys[m].at[:, columns], wide_k.at[place], w_sem.at[y * 2 + core, 0], z * 2 + to_y, m, own)
+            send(values[m].at[:, columns], wide_v.at[place], w_sem.at[y * 2 + core, 1], z * 2 + to_y, m, own)
+    for dz in range(layers):
+        for dy in range(2):
+            to_sp = lax.rem(z + dz, layers) * 2 + (y + dy) % 2
+            for m in range(2):
+                send(
+                    norm_send.at[m], norm_rows.at[me], norm_sem.at[me], to_sp, m,
+                    (core == m) if dz == 0 and dy == 0 else None,
+                )
+    token_rows = pl.ds(pl.multiple_of(sp * tokens, 16), tokens)
+    for b in range(per_half):
+        for to_y in range(2):
+            head = to_y * per_half + b
+            to_sp = (core * per_half + b) * 2 + to_y
+            for m in range(2):
+                own = (to_sp == sp) & (core == m)
+                send(
+                    queries[m].at[0, :, head * head_cols:(head + 1) * head_cols],
+                    query_rows.at[token_rows], q_sem.at[sp], to_sp, m, own,
+                )
+                send(documents.at[m], doc_rows.at[sp], doc_sem.at[sp], to_sp, m, own)
+
+    for dz in range(layers):
+        from_z = lax.rem(z - dz + layers, layers)
+        block = from_z * 2 + y
+        for c in range(2):
+            arrive(rows.at[block, c * tokens:(c + 1) * tokens], hid_sem.at[from_z, c])
+        send(rows.at[block], rows.at[block], fwd_sem.at[from_z], z * 2 + (1 - y), core, None)
+
+    for s in range(total):
+        arrive(norm_rows.at[s], norm_sem.at[s])
+    for s in range(4):
+        arrive(gain_rows.at[s], gain_sem.at[s])
+        arrive(wide_k.at[s * features:(s + 1) * features], w_sem.at[s, 0])
+        arrive(wide_v.at[s * features:(s + 1) * features], w_sem.at[s, 1])
+    gain_row = jnp.concatenate([gain_rows[s] for s in range(4)], axis=1)
+
+    for side in range(2):
+        for dz in range(layers):
+            from_z = lax.rem(z - dz + layers, layers)
+            block = from_z * 2 + (y + side) % 2
+            if side:
+                arrive(rows.at[block], fwd_sem.at[from_z])
+            scale = jnp.concatenate(
+                [
+                    jnp.sum(jnp.where(square, norm_rows[block * 2 + c], 0.0), axis=1, keepdims=True)
+                    for c in range(2)
+                ],
+                axis=0,
+            )
+            normed = (rows[block].astype(jnp.float32) * scale * gain_row).astype(jnp.bfloat16)
+            part_k = jnp.dot(normed, wide_k[...], preferred_element_type=jnp.float32)
+            part_v = jnp.dot(normed, wide_v[...], preferred_element_type=jnp.float32)
+            block_rows = pl.ds(pl.multiple_of(block * tokens, 16), tokens)
+            for s in range(2):
+                for b in range(per_half):
+                    to_z = s * per_half + b
+                    own = z == to_z
+                    picked = (slice(s * tokens, (s + 1) * tokens), slice(b * HEAD_DIM, (b + 1) * HEAD_DIM))
+                    slot = (side * layers + dz) * layers + to_z
+                    part_send[slot, :, :HEAD_DIM] = part_k[picked]
+                    part_send[slot, :, HEAD_DIM:] = part_v[picked]
+                    make = remote(
+                        part_send.at[slot], parts.at[z, block_rows], part_sem.at[z, block], to_z * 2 + y, core
+                    )
+                    away = jnp.logical_not(own)
+                    pending.append((away, make))
+
+                    @pl.when(away)
+                    def _(make=make):
+                        make().start()
+
+                    @pl.when(own)
+                    def _(slot=slot, block_rows=block_rows):
+                        parts[z, block_rows, :] = part_send[slot]
+
+    for s in range(sp_count):
+        arrive(query_rows.at[s * tokens:(s + 1) * tokens], q_sem.at[s])
+        arrive(doc_rows.at[s], doc_sem.at[s])
+        column = jnp.sum(jnp.where(square, doc_rows[s], 0.0), axis=1, keepdims=True)
+        doc_wide[s * tokens:(s + 1) * tokens, :] = jnp.broadcast_to(column, (tokens, 128))
+    query_index = lax.broadcasted_iota(jnp.int32, (length, length), 0)
+    key_index = lax.broadcasted_iota(jnp.int32, (length, length), 1)
+    doc_column = doc_wide[:, :1]
+    doc_row = jnp.sum(jnp.where(query_index == key_index, doc_column, 0.0), axis=0, keepdims=True)
+    allowed = (key_index <= query_index) & (doc_row == doc_column)
+
+    for from_z in range(layers):
+        @pl.when(z != from_z)
+        def _(from_z=from_z):
+            for s in range(sp_count):
+                arrive(parts.at[from_z, s * tokens:(s + 1) * tokens], part_sem.at[from_z, s])
+    raw = parts[0]
+    for from_z in range(1, layers):
+        raw = raw + parts[from_z]
+    raw_keys = raw[:, :HEAD_DIM]
+    key_heads = (
+        raw_keys * cosines[...] + pltpu.roll(raw_keys, HEAD_DIM // 2, 1) * sines[...]
+    ).astype(jnp.bfloat16)
+    value_heads = raw[:, HEAD_DIM:].astype(jnp.bfloat16)
+    factor = HEAD_DIM ** (-0.5)
+    for g in range(head_cols // HEAD_DIM):
+        columns = slice(g * HEAD_DIM, (g + 1) * HEAD_DIM)
+        scores = lax.dot_general(
+            query_rows[:, columns], key_heads, (((1,), (1,)), ((), ())), preferred_element_type=jnp.float32
+        ) * factor
+        scores = jnp.where(allowed, scores, MASKED)
+        highest = jnp.max(scores, axis=-1, keepdims=True)
+        exponent = jnp.where(allowed, jnp.exp(scores - highest), 0.0)
+        weights = (exponent / jnp.sum(exponent, axis=-1, keepdims=True)).astype(jnp.bfloat16)
+        mixed[:, columns] = jnp.dot(weights, value_heads, preferred_element_type=jnp.float32).astype(jnp.bfloat16)
+
+    my_seq, my_head = z // per_half, y * per_half + z % per_half
+    out_columns = pl.ds(pl.multiple_of(my_head * head_cols, 128), head_cols)
+    for s in range(sp_count):
+        send(
+            mixed.at[s * tokens:(s + 1) * tokens], out.at[core, :, out_columns],
+            out_sem.at[core, my_head], s, my_seq, (sp == s) & (core == my_seq),
+        )
+    for m in range(2):
+        for head in range(2 * per_half):
+            arrive(out.at[m, :, head * head_cols:(head + 1) * head_cols], out_sem.at[m, head])
+    for away, make in pending:
+        if away is None:
+            make().wait_send()
+        else:
+            @pl.when(away)
+            def _(make=make):
+                make().wait_send()
+
+
+def fused(mesh, hiddens, queries, documents, gains, keys, values):
+    sp = mesh.shape["sp"]
+    tokens, features = hiddens[0].shape[1], keys[0].shape[0]
+    kv_heads = keys[0].shape[1] // HEAD_DIM
+    head_cols = queries[0].shape[2] // kv_heads
+    layers, length, half = sp // 2, sp * tokens, keys[0].shape[1] // 2
+    half_dim = HEAD_DIM // 2
+    frequency = jnp.exp(
+        -jnp.log(ROPE_BASE) * jnp.arange(half_dim, dtype=jnp.float32) * 2.0 / HEAD_DIM
+    )
+    angles = jnp.arange(length, dtype=jnp.int32).astype(jnp.float32)[:, None] * frequency[None, :]
+    cosines, sines = jnp.cos(angles), jnp.sin(angles)
+    cosines = jnp.concatenate([cosines, cosines], axis=1)
+    sines = jnp.concatenate([-sines, sines], axis=1)
+    gain_pair = jnp.stack(gains)[:, None, :].astype(jnp.float32)
+    doc_pair = jnp.pad(jnp.stack(documents).astype(jnp.float32), ((0, 0), (0, 0), (0, 128 - tokens)))
+    dma = pltpu.SemaphoreType.DMA
+    bf16, f32 = jnp.bfloat16, jnp.float32
+    sends = 2 * layers + 12 + 4 * layers + 4 * kv_heads + layers + sp * layers + sp
+    out = pl.pallas_call(
+        functools.partial(fused_kernel, sp),
+        out_shape=jax.ShapeDtypeStruct((2, tokens, queries[0].shape[2]), bf16),
+        in_specs=[pl.BlockSpec(memory_space=pltpu.VMEM)] * 12,
+        out_specs=pl.BlockSpec(memory_space=pltpu.VMEM),
+        scratch_shapes=[
+            pltpu.VMEM((sp, 2 * tokens, 4 * features), bf16),
+            pltpu.VMEM((4 * features, half), bf16),
+            pltpu.VMEM((4 * features, half), bf16),
+            pltpu.VMEM((4, 1, features), f32),
+            pltpu.VMEM((2, 1, 128), f32),
+            pltpu.VMEM((2 * sp, 1, 128), f32),
+            pltpu.VMEM((length, head_cols), bf16),
+            pltpu.VMEM((sp, 1, 128), f32),
+            pltpu.VMEM((sp * layers, tokens, 2 * HEAD_DIM), f32),
+            pltpu.VMEM((layers, length, 2 * HEAD_DIM), f32),
+            pltpu.VMEM((length, 128), f32),
+            pltpu.VMEM((length, head_cols), bf16),
+            dma((sends,)),
+            dma((layers, 2)),
+            dma((layers,)),
+            dma((4, 2)),
+            dma((4,)),
+            dma((2 * sp,)),
+            dma((sp,)),
+            dma((sp,)),
+            dma((layers, sp)),
+            dma((2, kv_heads)),
+        ],
+        compiler_params=pltpu.CompilerParams(collective_id=0, has_side_effects=True),
+        name="fused",
+    )(*hiddens, *queries, *keys, *values, gain_pair, doc_pair, cosines, sines)
+    return (out[0][None], out[1][None])
+
+
 def per_device(
+    mesh,
     policy_hidden,
     policy_queries,
     policy_documents,
@@ -120,6 +422,16 @@
     frozen_key_weight,
     frozen_value_weight,
 ):
+    if fits(mesh, policy_hidden, policy_queries, policy_key_weight):
+        return fused(
+            mesh,
+            (policy_hidden, frozen_hidden),
+            (policy_queries, frozen_queries),
+            (policy_documents, frozen_documents),
+            (policy_gain, frozen_gain),
+            (policy_key_weight, frozen_key_weight),
+            (policy_value_weight, frozen_value_weight),
+        )
     policy_mixed = run_model(
         policy_hidden,
         policy_queries,
@@ -141,7 +453,7 @@
 
 def solution(mesh):
     return jax.shard_map(
-        per_device,
+        functools.partial(per_device, mesh),
         mesh=mesh,
         in_specs=(
             P(("groups", "fsdp"), "sp", None),

time: 282 us -> 61.4 us (0.22)
  waiting for transfers between devices: 145 us -> 0 us
  Pallas kernels: 0 us -> 54.5 us
  blocking collectives: 47.7 us -> 0 us
  starting transfers between devices: 30.9 us -> 0 us
  local copies, waits for them, and re-layouts: 26 us -> 4.08 us
  between operations: 14.7 us -> 0.66 us
  matrix products: 12.5 us -> 0 us
    all_gather x4 -> x0, waiting for transfers between devices: 107 us -> none  [the longest x2 73.7 us: project(): lax.all_gather(value_weight, ('sp', 'fsdp'), axis=0, tiled=True)]
    pallas_call x0 -> x1, Pallas kernels: none -> 54.5 us  [fused(): pl.pallas_call(functools.partial(fused_kernel, sp), out_shape=jax.ShapeDt...]
    all_gather x3 -> x0, blocking collectives: 47.7 us -> none  [the longest x2 39.6 us: project(): gain_rows = lax.all_gather(gain, ('sp', 'fsdp'), axis=0, tiled=True)]
    all_to_all x8 -> x0, waiting for transfers between devices: 35.3 us -> none  [the longest x2 11.1 us: run_model(): lax.all_to_all(mixed, 'sp', split_axis=0, concat_axis=1, tiled=True)]
    all_to_all x8 -> x0, starting transfers between devices: 30.8 us -> none  [the longest x2 10.7 us: run_model(): lax.all_to_all(query_local, 'sp', split_axis=1, concat_axis=0, tiled=True)]
    dot_general x2 -> x0, local copies, waits for them, and re-layouts: 12.8 us -> none  [project(): raw_keys = jnp.dot(normed, key_rows, preferred_element_type=jnp.float32)]
    dot_general x8 -> x0, matrix products: 12.5 us -> none  [the longest x2 6.11 us: project(): raw_values = jnp.dot(normed, value_rows, preferred_element_type=jnp.float32)]
    unnamed x23 -> x8, local copies, waits for them, and re-layouts: 7.46 us -> 1.97 us
  transfers between devices with their start and end apart: 12 -> 0, of which waited for: 9 -> 0; matrix products, arithmetic and copies ran while one was open for 14% -> 0% of each run, Pallas kernels for 0% -> 0%
where the time goes in v1:
time: 61.4 us; the launch traced here: 61.2 us
  Pallas kernels  54.5 us (89%)
  local copies, waits for them, and re-layouts  4.08 us (7%)
  other arithmetic  1.98 us (3%)
  between operations  0.66 us (1%)
    pallas_call x1, Pallas kernels, fused(): pl.pallas_call(functools.partial(fused_kernel, sp), out_shape=jax.ShapeDt...  54.5 us
    unnamed x8, local copies, waits for them, and re-layouts  1.97 us
    slice x1, local copies, waits for them, and re-layouts, fused(): return (out[0][None], out[1][None])  1.53 us

profile of v1, /device:TPU:0, one launch (start us, length us, event | category | flops | bytes accessed | tf_op | source)
XLA Modules:
  0.0 61.2 jit_solution(4571512896174807126)
XLA Ops:
  0.7 0.5 fusion
  1.2 0.8 %pad_maximum_fusion = (f32[256,128]{1,0:T(8,128)}, f32[256,128]{1,0:T(8,128)}) fusion(f32[256,64]{1,0:T(8,128)S(1)} %get-tuple-element.6, f32[256,64]{1,0:T(8,128)S(1)} %get-tuple-element.5, f32[256,64]{1,0:T(8,128)S(1)} %get-tuple-element.4), kind=kLoop, calls=%fused_computation.2 | loop fusion | flops 65536 | bytes 458752 | tf_op jit(solution)/shard_map/concatenate | solution.py:368
  2.0 0.0 copy-start.2
  2.0 0.7 %copy-done.2 = bf16[256]{0:T(256)(128)(2,1)S(1)} copy-done((bf16[256]{0:T(256)(128)(2,1)S(1)}, bf16[256]{0:T(256)(128)(2,1)}, u32[]{:S(2)}) %copy-start.2) | copy-done | bytes 536
  2.7 0.0 copy-start.3
  2.7 0.6 %copy-done.3 = bf16[256]{0:T(256)(128)(2,1)S(1)} copy-done((bf16[256]{0:T(256)(128)(2,1)S(1)}, bf16[256]{0:T(256)(128)(2,1)}, u32[]{:S(2)}) %copy-start.3) | copy-done | bytes 536
  3.4 0.6 maximum_convert_fusion.gains
  3.9 0.0 copy-start
  3.9 0.0 copy-start.1
  3.9 0.7 %copy-done = s32[1,32]{1,0:T(1,128)S(1)} copy-done((s32[1,32]{1,0:T(1,128)S(1)}, s32[1,32]{1,0:T(1,128)}, u32[]{:S(2)}) %copy-start) | copy-done | bytes 152
  4.6 0.0 copy-done.1
  4.6 0.6 pad.4.documents
  5.2 54.5 %fused.1 = bf16[2,32,1024]{2,1,0:T(8,128)(2,1)} custom-call(bf16[1,32,4096]{2,1,0:T(8,128)(2,1)} %hidden0.1, bf16[1,32,4096]{2,1,0:T(8,128)(2,1)} %hidden1.1, bf16[1,32,1024]{2,1,0:T(8,128)(2,1)} %queries0.1, bf16[1,32,1024]{2,1,0:T(8,128)(2,1)} %queries1.1, bf16[256,512]{1,0:T(8,128)(2,1)} %key0.1, bf16[256,512]{1,0:T(8,128)(2,1)} %key1.1, ...), custom_call_target="tpu_custom_call" | custom-call | tf_op jit(solution)/shard_map/fused/pallas_call | solution.py:375
  59.7 1.5 %fusion.1 = (bf16[1,32,1024]{2,1,0:T(8,128)(2,1)}, bf16[1,32,1024]{2,1,0:T(8,128)(2,1)}) fusion(bf16[2,32,1024]{2,1,0:T(8,128)(2,1)} %fused.1), kind=kLoop, calls=%fused_computation.9 | loop fusion | bytes 262144 | tf_op jit(solution)/shard_map/slice | solution.py:407
  (5 shorter events, 0.0 us)
Async XLA Ops:
  2.0 0.7 %copy-start.2 = (bf16[256]{0:T(256)(128)(2,1)S(1)}, bf16[256]{0:T(256)(128)(2,1)}, u32[]{:S(2)}) copy-start(bf16[256]{0:T(256)(128)(2,1)} %param.15) | copy-start | bytes 1540
  2.7 0.7 %copy-start.3 = (bf16[256]{0:T(256)(128)(2,1)S(1)}, bf16[256]{0:T(256)(128)(2,1)}, u32[]{:S(2)}) copy-start(bf16[256]{0:T(256)(128)(2,1)} %param.21) | copy-start | bytes 1540
  3.9 0.7 %copy-start = (s32[1,32]{1,0:T(1,128)S(1)}, s32[1,32]{1,0:T(1,128)}, u32[]{:S(2)}) copy-start(s32[1,32]{1,0:T(1,128)} %param.20) | copy-start | bytes 388
  3.9 0.7 %copy-start.1 = (s32[1,32]{1,0:T(1,128)S(1)}, s32[1,32]{1,0:T(1,128)}, u32[]{:S(2)}) copy-start(s32[1,32]{1,0:T(1,128)} %param.14) | copy-start | bytes 388

commit v2 on v1

--- a/solution.py
+++ b/solution.py
@@ -2,6 +2,7 @@
 
 import jax
 import jax.numpy as jnp
+import numpy as np
 from jax import lax
 from jax.experimental import pallas as pl
 from jax.experimental.pallas import tpu as pltpu
@@ -119,6 +120,7 @@
     kv_heads = key_weight.shape[1] // HEAD_DIM
     return (
         cores == 2
+        and mesh.shape["groups"] == 2
         and sp % 2 == 0
         and kv_heads % 2 == 0
         and sp // 2 == cores * (kv_heads // 2)
@@ -133,9 +135,9 @@
 def fused_kernel(
     sp_count,
     hidden0, hidden1, queries0, queries1, key0, key1, value0, value1,
-    gains, documents, cosines, sines,
-    out,
-    rows, wide_k, wide_v, gain_rows, norm_send, norm_rows, query_rows, doc_rows,
+    gain0, gain1, documents0, documents1, cosines, sines,
+    out0, out1,
+    rows, wide_k, wide_v, gains, documents, gain_rows, norm_send, norm_rows, query_rows, doc_rows,
     part_send, parts, doc_wide, mixed,
     send_sem, hid_sem, fwd_sem, w_sem, gain_sem, norm_sem, q_sem, doc_sem, part_sem, out_sem,
 ):
@@ -150,6 +152,7 @@
     layers = sp_count // 2
     sp, core = lax.axis_index("sp"), lax.axis_index("fsdp")
     z, y = sp // 2, sp % 2
+    group = lax.axis_index("groups")
     me = sp * 2 + core
     total = sp_count * 2
 
@@ -160,6 +163,8 @@
             barrier, inc=1, device_id={"sp": other // 2, "fsdp": other % 2}, device_id_type=MESH
         )
 
+    pl.semaphore_signal(barrier, inc=1, device_id={"groups": 1 - group}, device_id_type=MESH)
+
     square = (
         lax.broadcasted_iota(jnp.int32, (tokens, 128), 0)
         == lax.broadcasted_iota(jnp.int32, (tokens, 128), 1)
@@ -167,39 +172,42 @@
     for m in range(2):
         wide = hiddens[m][0].astype(jnp.float32)
         inverse = lax.rsqrt(jnp.mean(wide * wide, axis=-1, keepdims=True) + EPS)
+        gains[m] = (gain0, gain1)[m][...].astype(jnp.float32).reshape(1, -1)
+        documents[m] = jnp.zeros((1, 128), jnp.float32)
+        documents[m, :, :tokens] = (documents0, documents1)[m][...].astype(jnp.float32)
         norm_send[m] = jnp.sum(jnp.where(square, inverse, 0.0), axis=0, keepdims=True)
 
-    pl.semaphore_wait(barrier, total - 1)
+    pl.semaphore_wait(barrier, total)
 
     pending = []
 
-    def remote(src, dst, recv, to_sp, to_core):
+    def remote(src, dst, recv, target):
         slot = len(pending)
 
         def make():
             return pltpu.make_async_remote_copy(
                 src_ref=src, dst_ref=dst, send_sem=send_sem.at[slot], recv_sem=recv,
-                device_id={"sp": to_sp, "fsdp": to_core}, device_id_type=MESH,
+                device_id=target, device_id_type=MESH,
             )
 
         return make
 
+    def put(src, dst, recv, target, away):
+        make = remote(src, dst, recv, target)
+        pending.append((away, make))
+        if away is None:
+            make().start()
+        else:
+            @pl.when(away)
+            def _():
+                make().start()
+
     def send(src, dst, recv, to_sp, to_core, own):
-        make = remote(src, dst, recv, to_sp, to_core)
-        if own is None:
-            pending.append((None, make))
-            make().start()
-            return
-        away = jnp.logical_not(own)
-        pending.append((away, make))
-
-        @pl.when(away)
-        def _():
-            make().start()
-
-        @pl.when(own)
-        def _():
-            pltpu.make_async_copy(src, dst, recv).start()
+        put(src, dst, recv, {"sp": to_sp, "fsdp": to_core}, None if own is None else jnp.logical_not(own))
+        if own is not None:
+            @pl.when(own)
+            def _():
+                pltpu.make_async_copy(src, dst, recv).start()
 
     def arrive(dst, recv):
         pltpu.make_async_copy(dst, dst, recv).wait()
@@ -220,9 +228,14 @@
         columns = pl.ds(pl.multiple_of(to_y * half, 128), half)
         for m in range(2):
             own = (core == m) if dy == 0 else None
+            if dy:
+                target = {"sp": z * 2 + to_y, "fsdp": m}
+                put(keys[m].at[:, columns], wide_k.at[place], w_sem.at[y * 2 + core, 0], target, core == group)
+                put(values[m].at[:, columns], wide_v.at[place], w_sem.at[y * 2 + core, 1], target, core == group)
+            else:
+                send(keys[m].at[:, columns], wide_k.at[place], w_sem.at[y * 2 + core, 0], z * 2 + to_y, m, own)
+                send(values[m].at[:, columns], wide_v.at[place], w_sem.at[y * 2 + core, 1], z * 2 + to_y, m, own)
             send(gains.at[m], gain_rows.at[y * 2 + core], gain_sem.at[y * 2 + core], z * 2 + to_y, m, own)
-            send(keys[m].at[:, columns], wide_k.at[place], w_sem.at[y * 2 + core, 0], z * 2 + to_y, m, own)
-            send(values[m].at[:, columns], wide_v.at[place], w_sem.at[y * 2 + core, 1], z * 2 + to_y, m, own)
     for dz in range(layers):
         for dy in range(2):
             to_sp = lax.rem(z + dz, layers) * 2 + (y + dy) % 2
@@ -250,13 +263,20 @@
         for c in range(2):
             arrive(rows.at[block, c * tokens:(c + 1) * tokens], hid_sem.at[from_z, c])
         send(rows.at[block], rows.at[block], fwd_sem.at[from_z], z * 2 + (1 - y), core, None)
+        if dz < 2:
+            source = (1 - y) * 2 + group
+            wide = (wide_k, wide_v)[dz].at[pl.ds(pl.multiple_of(source * features, 128), features)]
+            arrive(wide, w_sem.at[source, dz])
+            put(wide, wide, w_sem.at[source, dz], {"groups": 1 - group}, None)
 
     for s in range(total):
         arrive(norm_rows.at[s], norm_sem.at[s])
     for s in range(4):
         arrive(gain_rows.at[s], gain_sem.at[s])
-        arrive(wide_k.at[s * features:(s + 1) * features], w_sem.at[s, 0])
-        arrive(wide_v.at[s * features:(s + 1) * features], w_sem.at[s, 1])
+    for source in (y * 2, y * 2 + 1, (1 - y) * 2 + 1 - group):
+        place = pl.ds(pl.multiple_of(source * features, 128), features)
+        arrive(wide_k.at[place], w_sem.at[source, 0])
+        arrive(wide_v.at[place], w_sem.at[source, 1])
     gain_row = jnp.concatenate([gain_rows[s] for s in range(4)], axis=1)
 
     for side in range(2):
@@ -285,7 +305,8 @@
                     part_send[slot, :, :HEAD_DIM] = part_k[picked]
                     part_send[slot, :, HEAD_DIM:] = part_v[picked]
                     make = remote(
-                        part_send.at[slot], parts.at[z, block_rows], part_sem.at[z, block], to_z * 2 + y, core
+                        part_send.at[slot], parts.at[z, block_rows], part_sem.at[z, block],
+                        {"sp": to_z * 2 + y, "fsdp": core},
                     )
                     away = jnp.logical_not(own)
                     pending.append((away, make))
@@ -323,7 +344,10 @@
     ).astype(jnp.bfloat16)
     value_heads = raw[:, HEAD_DIM:].astype(jnp.bfloat16)
     factor = HEAD_DIM ** (-0.5)
-    for g in range(head_cols // HEAD_DIM):
+    my_seq, my_head = z // per_half, y * per_half + z % per_half
+    group_size = head_cols // HEAD_DIM
+    outs = (out0, out1)
+    for g in range(group_size):
         columns = slice(g * HEAD_DIM, (g + 1) * HEAD_DIM)
         scores = lax.dot_general(
             query_rows[:, columns], key_heads, (((1,), (1,)), ((), ())), preferred_element_type=jnp.float32
@@ -332,18 +356,22 @@
         highest = jnp.max(scores, axis=-1, keepdims=True)
         exponent = jnp.where(allowed, jnp.exp(scores - highest), 0.0)
         weights = (exponent / jnp.sum(exponent, axis=-1, keepdims=True)).astype(jnp.bfloat16)
-        mixed[:, columns] = jnp.dot(weights, value_heads, preferred_element_type=jnp.float32).astype(jnp.bfloat16)
-
-    my_seq, my_head = z // per_half, y * per_half + z % per_half
-    out_columns = pl.ds(pl.multiple_of(my_head * head_cols, 128), head_cols)
-    for s in range(sp_count):
-        send(
-            mixed.at[s * tokens:(s + 1) * tokens], out.at[core, :, out_columns],
-            out_sem.at[core, my_head], s, my_seq, (sp == s) & (core == my_seq),
-        )
+        mixed[g] = jnp.dot(weights, value_heads, preferred_element_type=jnp.float32).astype(jnp.bfloat16)
+        head = my_head * group_size + g
+        out_columns = pl.ds(pl.multiple_of(head * HEAD_DIM, 128), HEAD_DIM)
+        for s in range(sp_count):
+            own = (sp == s) & (core == my_seq)
+            for m in range(2):
+                src = mixed.at[g, s * tokens:(s + 1) * tokens]
+                dst, recv = outs[m].at[0, :, out_columns], out_sem.at[m, head]
+                put(src, dst, recv, {"sp": s, "fsdp": my_seq}, (core == m) & jnp.logical_not(own))
+
+                @pl.when((core == m) & own)
+                def _(src=src, dst=dst, recv=recv):
+                    pltpu.make_async_copy(src, dst, recv).start()
     for m in range(2):
-        for head in range(2 * per_half):
-            arrive(out.at[m, :, head * head_cols:(head + 1) * head_cols], out_sem.at[m, head])
+        for head in range(2 * per_half * group_size):
+            arrive(outs[m].at[0, :, head * HEAD_DIM:(head + 1) * HEAD_DIM], out_sem.at[m, head])
     for away, make in pending:
         if away is None:
             make().wait_send()
@@ -360,27 +388,26 @@
     head_cols = queries[0].shape[2] // kv_heads
     layers, length, half = sp // 2, sp * tokens, keys[0].shape[1] // 2
     half_dim = HEAD_DIM // 2
-    frequency = jnp.exp(
-        -jnp.log(ROPE_BASE) * jnp.arange(half_dim, dtype=jnp.float32) * 2.0 / HEAD_DIM
-    )
-    angles = jnp.arange(length, dtype=jnp.int32).astype(jnp.float32)[:, None] * frequency[None, :]
-    cosines, sines = jnp.cos(angles), jnp.sin(angles)
-    cosines = jnp.concatenate([cosines, cosines], axis=1)
-    sines = jnp.concatenate([-sines, sines], axis=1)
-    gain_pair = jnp.stack(gains)[:, None, :].astype(jnp.float32)
-    doc_pair = jnp.pad(jnp.stack(documents).astype(jnp.float32), ((0, 0), (0, 0), (0, 128 - tokens)))
+    frequency = ROPE_BASE ** (-2.0 * np.arange(half_dim) / HEAD_DIM)
+    angles = np.arange(length)[:, None] * frequency[None, :]
+    cosines = np.concatenate([np.cos(angles), np.cos(angles)], axis=1).astype(np.float32)
+    sines = np.concatenate([-np.sin(angles), np.sin(angles)], axis=1).astype(np.float32)
     dma = pltpu.SemaphoreType.DMA
     bf16, f32 = jnp.bfloat16, jnp.float32
-    sends = 2 * layers + 12 + 4 * layers + 4 * kv_heads + layers + sp * layers + sp
-    out = pl.pallas_call(
+    sends = 2 * layers + 12 + 4 * layers + 4 * kv_heads + layers + sp * layers
+    group_size = head_cols // HEAD_DIM
+    sends = sends + 2 + 2 * group_size * sp
+    return pl.pallas_call(
         functools.partial(fused_kernel, sp),
-        out_shape=jax.ShapeDtypeStruct((2, tokens, queries[0].shape[2]), bf16),
-        in_specs=[pl.BlockSpec(memory_space=pltpu.VMEM)] * 12,
-        out_specs=pl.BlockSpec(memory_space=pltpu.VMEM),
+        out_shape=(jax.ShapeDtypeStruct((1, tokens, queries[0].shape[2]), bf16),) * 2,
+        in_specs=[pl.BlockSpec(memory_space=pltpu.VMEM)] * 14,
+        out_specs=(pl.BlockSpec(memory_space=pltpu.VMEM),) * 2,
         scratch_shapes=[
             pltpu.VMEM((sp, 2 * tokens, 4 * features), bf16),
             pltpu.VMEM((4 * features, half), bf16),
             pltpu.VMEM((4 * features, half), bf16),
+            pltpu.VMEM((2, 1, features), f32),
+            pltpu.VMEM((2, 1, 128), f32),
             pltpu.VMEM((4, 1, features), f32),
             pltpu.VMEM((2, 1, 128), f32),
             pltpu.VMEM((2 * sp, 1, 128), f32),
@@ -389,7 +416,7 @@
             pltpu.VMEM((sp * layers, tokens, 2 * HEAD_DIM), f32),
             pltpu.VMEM((layers, length, 2 * HEAD_DIM), f32),
             pltpu.VMEM((length, 128), f32),
-            pltpu.VMEM((length, head_cols), bf16),
+            pltpu.VMEM((group_size, length, HEAD_DIM), bf16),
             dma((sends,)),
             dma((layers, 2)),
             dma((layers,)),
@@ -399,12 +426,14 @@
             dma((sp,)),
             dma((sp,)),
             dma((layers, sp)),
-            dma((2, kv_heads)),
+            dma((2, kv_heads * group_size)),
         ],
         compiler_params=pltpu.CompilerParams(collective_id=0, has_side_effects=True),
         name="fused",
-    )(*hiddens, *queries, *keys, *values, gain_pair, doc_pair, cosines, sines)
-    return (out[0][None], out[1][None])
+    )(
+        *hiddens, *queries, *keys, *values,
+        *gains, *documents, cosines, sines,
+    )
 
 
 def per_device(

time: 61.4 us -> 58.4 us (0.951)
  other arithmetic: 1.98 us -> 0 us
  local copies, waits for them, and re-layouts: 4.08 us -> 2.14 us
  Pallas kernels: 54.5 us -> 55.4 us
    slice x1 -> x0, local copies, waits for them, and re-layouts: 1.53 us -> none  [fused(): return (out[0][None], out[1][None])]
    pallas_call x1, Pallas kernels: 54.5 us -> 55.4 us  [fused(): pl.pallas_call(functools.partial(fused_kernel, sp), out_shape=(jax.ShapeD...]
    concatenate x1 -> x0, other arithmetic: 0.84 us -> none  [fused(): cosines = jnp.concatenate([cosines, cosines], axis=1)]
    unnamed x8 -> x4, local copies, waits for them, and re-layouts: 1.97 us -> 2.14 us
where the time goes in v2:
time: 58.4 us; the launch traced here: 58.2 us
  Pallas kernels  55.4 us (95%)
  local copies, waits for them, and re-layouts  2.14 us (4%)
  between operations  0.65 us (1%)
    pallas_call x1, Pallas kernels, fused(): pl.pallas_call(functools.partial(fused_kernel, sp), out_shape=(jax.ShapeD...  55.4 us
    unnamed x4, local copies, waits for them, and re-layouts  2.14 us

profile of v2, /device:TPU:0, one launch (start us, length us, event | category | flops | bytes accessed | tf_op | source)
XLA Modules:
  0.0 58.2 jit_solution(8041392765946052701)
XLA Ops:
  0.6 55.4 %fused.1 = (bf16[1,32,1024]{2,1,0:T(8,128)(2,1)}, bf16[1,32,1024]{2,1,0:T(8,128)(2,1)}) custom-call(bf16[1,32,4096]{2,1,0:T(8,128)(2,1)} %hidden0.1, bf16[1,32,4096]{2,1,0:T(8,128)(2,1)} %hidden1.1, bf16[1,32,1024]{2,1,0:T(8,128)(2,1)} %queries0.1, bf16[1,32,1024]{2,1,0:T(8,128)(2,1)} %queries1.1, bf16[256,512]{1,0:T(8,128)(2,1)} %key0.1, ...), custom_call_target="tpu_custom_call" | custom-call | tf_op jit(solution)/shard_map/fused/pallas_call | solution.py:400
  56.0 0.0 copy-start
  56.1 1.5 %copy.18 = bf16[1,32,1024]{2,1,0:T(8,128)(2,1)} copy(bf16[1,32,1024]{2,1,0:T(8,128)(2,1)} %get-tuple-element.4) | data formatting | bytes 131072
  57.6 0.0 copy-done
  57.6 0.6 %copy.19 = bf16[1,32,1024]{2,1,0:T(8,128)(2,1)} copy(bf16[1,32,1024]{2,1,0:T(8,128)(2,1)S(1)} %copy-done) | data formatting | bytes 131072
Async XLA Ops:
  56.0 1.5 %copy-start = (bf16[1,32,1024]{2,1,0:T(8,128)(2,1)S(1)}, bf16[1,32,1024]{2,1,0:T(8,128)(2,1)}, u32[]{:S(2)}) copy-start(bf16[1,32,1024]{2,1,0:T(8,128)(2,1)} %get-tuple-element.5) | copy-start | bytes 196612

commit v3 on v2

--- a/solution.py
+++ b/solution.py
@@ -9,6 +9,7 @@
 from jax.sharding import PartitionSpec as P
 
 HEAD_DIM = 128
+LAG = 2
 
 
 EPS = 1e-05
@@ -123,6 +124,7 @@
         and mesh.shape["groups"] == 2
         and sp % 2 == 0
         and kv_heads % 2 == 0
+        and kv_heads == 4
         and sp // 2 == cores * (kv_heads // 2)
         and queries.shape[2] % (kv_heads * HEAD_DIM) == 0
         and key_weight.shape[0] % 128 == 0
@@ -137,9 +139,9 @@
     hidden0, hidden1, queries0, queries1, key0, key1, value0, value1,
     gain0, gain1, documents0, documents1, cosines, sines,
     out0, out1,
-    rows, wide_k, wide_v, gains, documents, gain_rows, norm_send, norm_rows, query_rows, doc_rows,
-    part_send, parts, doc_wide, mixed,
-    send_sem, hid_sem, fwd_sem, w_sem, gain_sem, norm_sem, q_sem, doc_sem, part_sem, out_sem,
+    near, near_sem, rows, wide_k, wide_v, gains, documents, gain_rows, norm_send, norm_rows, query_rows, doc_rows,
+    part_send, relayed, parts, doc_wide, mixed,
+    send_sem, hid_sem, fwd_sem, w_sem, gain_sem, norm_sem, q_sem, doc_sem, part_sem, relay_sem, out_sem,
 ):
     hiddens, queries = (hidden0, hidden1), (queries0, queries1)
     keys, values = (key0, key1), (value0, value1)
@@ -156,6 +158,8 @@
     me = sp * 2 + core
     total = sp_count * 2
 
+    for m in range(2):
+        pltpu.make_async_copy(hiddens[m].at[0], near.at[m], near_sem.at[m]).start()
     barrier = pltpu.get_barrier_semaphore()
     for step in range(1, total):
         other = lax.rem(me + step, total)
@@ -170,7 +174,8 @@
         == lax.broadcasted_iota(jnp.int32, (tokens, 128), 1)
     )
     for m in range(2):
-        wide = hiddens[m][0].astype(jnp.float32)
+        pltpu.make_async_copy(hiddens[m].at[0], near.at[m], near_sem.at[m]).wait()
+        wide = near[m].astype(jnp.float32)
         inverse = lax.rsqrt(jnp.mean(wide * wide, axis=-1, keepdims=True) + EPS)
         gains[m] = (gain0, gain1)[m][...].astype(jnp.float32).reshape(1, -1)
         documents[m] = jnp.zeros((1, 128), jnp.float32)
@@ -279,45 +284,68 @@
         arrive(wide_v.at[place], w_sem.at[source, 1])
     gain_row = jnp.concatenate([gain_rows[s] for s in range(4)], axis=1)
 
-    for side in range(2):
-        for dz in range(layers):
-            from_z = lax.rem(z - dz + layers, layers)
-            block = from_z * 2 + (y + side) % 2
-            if side:
-                arrive(rows.at[block], fwd_sem.at[from_z])
-            scale = jnp.concatenate(
-                [
-                    jnp.sum(jnp.where(square, norm_rows[block * 2 + c], 0.0), axis=1, keepdims=True)
-                    for c in range(2)
-                ],
-                axis=0,
+    inner = (z == per_half - 1) | (z == per_half)
+    outer = jnp.logical_not(inner)
+    neighbour = per_half - 1 + z // per_half
+
+    def onward(index):
+        block = (index % layers) * 2 + (y + index // layers) % 2
+        block_rows = pl.ds(pl.multiple_of(block * tokens, 16), tokens)
+        for to_z in range(layers):
+            slot = index * layers + to_z
+            away = inner & (z // per_half != to_z // per_half)
+
+            @pl.when(away)
+            def _(slot=slot):
+                arrive(relayed.at[slot], relay_sem.at[slot])
+                part_send[slot] = part_send[slot] + relayed[slot]
+
+            put(
+                part_send.at[slot], parts.at[z, block_rows], part_sem.at[z, block],
+                {"sp": to_z * 2 + y, "fsdp": core}, away,
             )
-            normed = (rows[block].astype(jnp.float32) * scale * gain_row).astype(jnp.bfloat16)
-            part_k = jnp.dot(normed, wide_k[...], preferred_element_type=jnp.float32)
-            part_v = jnp.dot(normed, wide_v[...], preferred_element_type=jnp.float32)
-            block_rows = pl.ds(pl.multiple_of(block * tokens, 16), tokens)
-            for s in range(2):
-                for b in range(per_half):
-                    to_z = s * per_half + b
-                    own = z == to_z
-                    picked = (slice(s * tokens, (s + 1) * tokens), slice(b * HEAD_DIM, (b + 1) * HEAD_DIM))
-                    slot = (side * layers + dz) * layers + to_z
-                    part_send[slot, :, :HEAD_DIM] = part_k[picked]
-                    part_send[slot, :, HEAD_DIM:] = part_v[picked]
-                    make = remote(
-                        part_send.at[slot], parts.at[z, block_rows], part_sem.at[z, block],
-                        {"sp": to_z * 2 + y, "fsdp": core},
-                    )
-                    away = jnp.logical_not(own)
-                    pending.append((away, make))
-
-                    @pl.when(away)
-                    def _(make=make):
-                        make().start()
-
-                    @pl.when(own)
-                    def _(slot=slot, block_rows=block_rows):
-                        parts[z, block_rows, :] = part_send[slot]
+
+    for index in range(2 * layers):
+        from_z, side = index % layers, index // layers
+        block = from_z * 2 + (y + side) % 2
+        if side:
+            arrive(rows.at[block], fwd_sem.at[from_z])
+        scale = jnp.concatenate(
+            [
+                jnp.sum(jnp.where(square, norm_rows[block * 2 + c], 0.0), axis=1, keepdims=True)
+                for c in range(2)
+            ],
+            axis=0,
+        )
+        normed = (rows[block].astype(jnp.float32) * scale * gain_row).astype(jnp.bfloat16)
+        part_k = jnp.dot(normed, wide_k[...], preferred_element_type=jnp.float32)
+        part_v = jnp.dot(normed, wide_v[...], preferred_element_type=jnp.float32)
+        block_rows = pl.ds(pl.multiple_of(block * tokens, 16), tokens)
+        for s in range(2):
+            for b in range(per_half):
+                to_z = s * per_half + b
+                same = z // per_half == s
+                picked = (slice(s * tokens, (s + 1) * tokens), slice(b * HEAD_DIM, (b + 1) * HEAD_DIM))
+                slot = index * layers + to_z
+                part_send[slot, :, :HEAD_DIM] = part_k[picked]
+                part_send[slot, :, HEAD_DIM:] = part_v[picked]
+                put(
+                    part_send.at[slot], parts.at[z, block_rows], part_sem.at[z, block],
+                    {"sp": to_z * 2 + y, "fsdp": core}, same & (z != to_z),
+                )
+                put(
+                    part_send.at[slot], relayed.at[slot], relay_sem.at[slot],
+                    {"sp": neighbour * 2 + y, "fsdp": core}, outer & jnp.logical_not(same),
+                )
+
+                @pl.when(z == to_z)
+                def _(slot=slot, block_rows=block_rows):
+                    parts[z, block_rows, :] = part_send[slot]
+
+        if index >= LAG:
+            onward(index - LAG)
+    for index in range(2 * layers - LAG, 2 * layers):
+        onward(index)
 
     for s in range(sp_count):
         arrive(query_rows.at[s * tokens:(s + 1) * tokens], q_sem.at[s])
@@ -330,14 +358,17 @@
     doc_row = jnp.sum(jnp.where(query_index == key_index, doc_column, 0.0), axis=0, keepdims=True)
     allowed = (key_index <= query_index) & (doc_row == doc_column)
 
+    def sent_by(from_z):
+        if from_z in (per_half - 1, per_half):
+            return z != from_z
+        return (z != from_z) & (z // per_half == from_z // per_half)
+
     for from_z in range(layers):
-        @pl.when(z != from_z)
+        @pl.when(sent_by(from_z))
         def _(from_z=from_z):
             for s in range(sp_count):
                 arrive(parts.at[from_z, s * tokens:(s + 1) * tokens], part_sem.at[from_z, s])
-    raw = parts[0]
-    for from_z in range(1, layers):
-        raw = raw + parts[from_z]
+    raw = parts[z] + parts[z + 1 - 2 * (z % 2)] + parts[per_half - z // per_half]
     raw_keys = raw[:, :HEAD_DIM]
     key_heads = (
         raw_keys * cosines[...] + pltpu.roll(raw_keys, HEAD_DIM // 2, 1) * sines[...]
@@ -396,13 +427,15 @@
     bf16, f32 = jnp.bfloat16, jnp.float32
     sends = 2 * layers + 12 + 4 * layers + 4 * kv_heads + layers + sp * layers
     group_size = head_cols // HEAD_DIM
-    sends = sends + 2 + 2 * group_size * sp
+    sends = sends + 2 + 2 * group_size * sp + 2 * sp * layers
     return pl.pallas_call(
         functools.partial(fused_kernel, sp),
         out_shape=(jax.ShapeDtypeStruct((1, tokens, queries[0].shape[2]), bf16),) * 2,
-        in_specs=[pl.BlockSpec(memory_space=pltpu.VMEM)] * 14,
+        in_specs=[pl.BlockSpec(memory_space=pl.ANY)] * 8 + [pl.BlockSpec(memory_space=pltpu.VMEM)] * 6,
         out_specs=(pl.BlockSpec(memory_space=pltpu.VMEM),) * 2,
         scratch_shapes=[
+            pltpu.VMEM((2,) + hiddens[0].shape[1:], bf16),
+            dma((2,)),
             pltpu.VMEM((sp, 2 * tokens, 4 * features), bf16),
             pltpu.VMEM((4 * features, half), bf16),
             pltpu.VMEM((4 * features, half), bf16),
@@ -413,6 +446,7 @@
             pltpu.VMEM((2 * sp, 1, 128), f32),
             pltpu.VMEM((length, head_cols), bf16),
             pltpu.VMEM((sp, 1, 128), f32),
+            pltpu.VMEM((sp * layers, tokens, 2 * HEAD_DIM), f32),
             pltpu.VMEM((sp * layers, tokens, 2 * HEAD_DIM), f32),
             pltpu.VMEM((layers, length, 2 * HEAD_DIM), f32),
             pltpu.VMEM((length, 128), f32),
@@ -426,6 +460,7 @@
             dma((sp,)),
             dma((sp,)),
             dma((layers, sp)),
+            dma((sp * layers,)),
             dma((2, kv_heads * group_size)),
         ],
         compiler_params=pltpu.CompilerParams(collective_id=0, has_side_effects=True),

time: 58.4 us -> 56.2 us (0.962)
  Pallas kernels: 55.4 us -> 53.2 us
    pallas_call x1, Pallas kernels: 55.4 us -> 53.2 us  [fused(): pl.pallas_call(functools.partial(fused_kernel, sp), out_shape=(jax.ShapeD...]
where the time goes in v3:
time: 56.2 us; the launch traced here: 56 us
  Pallas kernels  53.2 us (95%)
  local copies, waits for them, and re-layouts  2.14 us (4%)
  between operations  0.65 us (1%)
    pallas_call x1, Pallas kernels, fused(): pl.pallas_call(functools.partial(fused_kernel, sp), out_shape=(jax.ShapeD...  53.2 us
    unnamed x4, local copies, waits for them, and re-layouts  2.14 us

profile of v3, /device:TPU:0, one launch (start us, length us, event | category | flops | bytes accessed | tf_op | source)
XLA Modules:
  0.0 56.0 jit_solution(8535611271527436598)
XLA Ops:
  0.6 53.2 %fused.1 = (bf16[1,32,1024]{2,1,0:T(8,128)(2,1)}, bf16[1,32,1024]{2,1,0:T(8,128)(2,1)}) custom-call(bf16[1,32,4096]{2,1,0:T(8,128)(2,1)} %hidden0.1, bf16[1,32,4096]{2,1,0:T(8,128)(2,1)} %hidden1.1, bf16[1,32,1024]{2,1,0:T(8,128)(2,1)} %queries0.1, bf16[1,32,1024]{2,1,0:T(8,128)(2,1)} %queries1.1, bf16[256,512]{1,0:T(8,128)(2,1)} %key0.1, ...), custom_call_target="tpu_custom_call" | custom-call | tf_op jit(solution)/shard_map/fused/pallas_call | solution.py:431
  53.9 0.0 copy-start
  53.9 1.5 %copy.18 = bf16[1,32,1024]{2,1,0:T(8,128)(2,1)} copy(bf16[1,32,1024]{2,1,0:T(8,128)(2,1)} %get-tuple-element.4) | data formatting | bytes 131072
  55.4 0.0 copy-done
  55.4 0.6 %copy.19 = bf16[1,32,1024]{2,1,0:T(8,128)(2,1)} copy(bf16[1,32,1024]{2,1,0:T(8,128)(2,1)S(1)} %copy-done) | data formatting | bytes 131072
Async XLA Ops:
  53.9 1.5 %copy-start = (bf16[1,32,1024]{2,1,0:T(8,128)(2,1)S(1)}, bf16[1,32,1024]{2,1,0:T(8,128)(2,1)}, u32[]{:S(2)}) copy-start(bf16[1,32,1024]{2,1,0:T(8,128)(2,1)} %get-tuple-element.5) | copy-start | bytes 196612
